TPU v7x, 32 devices: a whole 2x2x4 slice. The times are simulated.
32 devices in a mesh: task: 8 (over z, y), aux: 4 (over x, core).
Axes of the slice: x: 2, y: 2, z: 4, core: 2. Of those that a mesh axis runs over, the one named last changes fastest.
Arguments:
- factors: bfloat16 [8, 2048, 1024], P('task', 'aux'), may hold values from -0.125 to 0.125
- amplitudes: bfloat16 [8, 256, 1024], P('task'), may hold values from -6 to 6
- task_counts: int32 [8], P('task'), may hold values from 1 to 4, 16 in all
- task_tiles: int32 [8, 4, 3], P('task'), may hold values from 0 to 4
Outputs:
- residual: float32 [8, 256, 1024], P('task', None, 'aux')
Inputs may be any that keep to these rules, and one draw needn't show every extreme that they name: `task_counts`: every tile has 1 to 4 tasks, exactly 16 in all; some tile has exactly 4.
All inputs are finite; a program needn't handle non-finite values. No bound on the sum of `task_counts` on one device may be relied on, other than what follows from the above.
Results may differ from a plain program's by a relative error of at most 0.0026.
Values may be sent and summed in bfloat16 or wider, within the bound.
A program may use at most 64 MiB of HBM per device.

v0:
```python
import jax
import jax.numpy as jnp
from jax import lax
from jax.experimental import pallas as pl
from jax.experimental.pallas import tpu as pltpu
from jax.sharding import PartitionSpec as P

VB = 32
RADIUS = 2
SPAN = 2 * RADIUS + 1
LANES = 128
SPREAD = LANES // VB
STEP = 2


def shifted(block, axis, distance):
    devices = range(lax.axis_size(axis))
    route = [((i - distance) % len(devices), i) for i in devices]
    return lax.ppermute(block, axis, route)


def swap_matrix(width):
    pairs = width * width
    rows = lax.broadcasted_iota(jnp.int32, (pairs, pairs), 0)
    cols = lax.broadcasted_iota(jnp.int32, (pairs, pairs), 1)
    return (rows == (cols % width) * width + cols // width).astype(jnp.bfloat16)


def roll_groups(x, amount):
    if amount == 0:
        return x
    parts = [
        pltpu.roll(x[:, j * LANES : (j + 1) * LANES], amount, 1)
        for j in range(x.shape[1] // LANES)
    ]
    return jnp.concatenate(parts, axis=1)


def kernel(counts, plan, swap, *refs):
    fac_in, amp_in = refs[:SPAN], refs[SPAN : 2 * SPAN]
    out, fac, amp, flip, tile, sems = refs[2 * SPAN :]
    pairs = swap.shape[0]
    blocks = pairs // LANES
    copies = [pltpu.make_async_copy(fac_in[i], fac.at[i], sems.at[i]) for i in range(SPAN)]
    copies += [
        pltpu.make_async_copy(amp_in[i], amp.at[i], sems.at[SPAN + i]) for i in range(SPAN)
    ]
    for copy in copies:
        copy.start()
    out[...] = jnp.zeros_like(out)
    for copy in copies:
        copy.wait()
    lanes = STEP * LANES
    group = (lax.broadcasted_iota(jnp.int32, (VB * blocks, lanes), 1) // VB) % SPREAD

    @pl.loop(0, counts[0])
    def _(slot):
        left, right, third = plan[slot, 0], plan[slot, 1], plan[slot, 2]
        for a_hi in range(blocks):
            strip = fac[left, :, a_hi * LANES : (a_hi + 1) * LANES].T
            for s in range(SPREAD):
                flip[s, a_hi * VB : (a_hi + 1) * VB, :] = strip[s * VB : (s + 1) * VB, :]

        @pl.loop(0, blocks // STEP)
        def _(step):
            base = pl.multiple_of(step * lanes, lanes)
            cols = swap[:, pl.ds(base, lanes)]
            swapped = jnp.dot(fac[right], cols, preferred_element_type=jnp.float32)
            outs = []
            for s in range(SPREAD):
                turned = roll_groups(swapped, s * VB).astype(jnp.bfloat16)
                outs.append(jnp.dot(flip[s], turned, preferred_element_type=jnp.float32))
            for t in range(SPREAD):
                mixed = outs[(SPREAD - 1 - t) % SPREAD]
                for g in range(SPREAD - 1):
                    mixed = jnp.where(group == g, outs[(g - t) % SPREAD], mixed)
                mixed = roll_groups(mixed, (LANES - t * VB) % LANES).astype(jnp.bfloat16)
                for j in range(STEP):
                    row = pl.multiple_of(base + (j * SPREAD + t) * VB, VB)
                    for a_hi in range(blocks):
                        tile[pl.ds(row, VB), a_hi * LANES : (a_hi + 1) * LANES] = mixed[
                            a_hi * VB : (a_hi + 1) * VB, j * LANES : (j + 1) * LANES
                        ]

        @pl.loop(0, blocks // STEP)
        def _(step):
            base = pl.multiple_of(step * lanes, lanes)
            amps = jnp.dot(
                amp[third], swap[:, pl.ds(base, lanes)], preferred_element_type=jnp.float32
            ).astype(jnp.bfloat16)
            out[...] += jnp.dot(
                amps, tile[pl.ds(base, lanes), :], preferred_element_type=jnp.float32
            )


def run_tasks(facs, amps, counts, plan):
    depth, pairs = facs[0].shape
    occ = amps[0].shape[0]
    anywhere = pl.BlockSpec(memory_space=pl.ANY)
    scalars = pl.BlockSpec(memory_space=pltpu.SMEM)
    return pl.pallas_call(
        kernel,
        out_shape=jax.ShapeDtypeStruct((occ, pairs), jnp.float32),
        in_specs=[scalars, scalars, pl.BlockSpec(memory_space=pltpu.VMEM)]
        + [anywhere] * (2 * SPAN),
        out_specs=pl.BlockSpec(memory_space=pltpu.VMEM),
        scratch_shapes=[
            pltpu.VMEM((SPAN, depth, pairs), jnp.bfloat16),
            pltpu.VMEM((SPAN, occ, pairs), jnp.bfloat16),
            pltpu.VMEM((SPREAD, pairs // SPREAD, depth), jnp.bfloat16),
            pltpu.VMEM((pairs, pairs), jnp.bfloat16),
            pltpu.SemaphoreType.DMA((2 * SPAN,)),
        ],
        compiler_params=pltpu.CompilerParams(vmem_limit_bytes=48 * 1024 * 1024),
    )(counts, plan, swap_matrix(VB), *facs, *amps)


def shards(factors, amplitudes, task_counts, task_tiles):
    own_fac = factors[0]
    own_amp = amplitudes[0]
    facs = []
    amps = []
    for offset in range(-RADIUS, RADIUS + 1):
        if offset == 0:
            facs.append(own_fac)
            amps.append(own_amp)
        else:
            moved = shifted((own_fac, own_amp), "task", -offset)
            facs.append(moved[0])
            amps.append(moved[1])
    partial_sum = run_tasks(facs, amps, task_counts, task_tiles[0])
    summed = lax.psum_scatter(partial_sum, "aux", scatter_dimension=1, tiled=True)
    return summed[None]


def solution(mesh):
    return jax.shard_map(
        shards,
        mesh=mesh,
        in_specs=(P("task", "aux", None), P("task", None, None), P("task"), P("task", None, None)),
        out_specs=P("task", None, "aux"),
        check_vma=False,
    )
```

profile of v0, /device:TPU:1, one launch (start us, length us, event | category | flops | bytes accessed | tf_op | source)
XLA Modules:
  0.0 187.0 jit_solution(13917026145621492430)
XLA Ops:
  6.5 0.0 reduce-scatter.2.cloned.1.call-start
  6.5 4.1 %collective-permute-start.7 = (bf16[256,1024]{1,0:T(8,128)(2,1)}, bf16[256,1024]{1,0:T(8,128)(2,1)S(1)}, u32[]{:S(2)}, u32[]{:S(2)}) collective-permute-start(bf16[256,1024]{1,0:T(8,128)(2,1)} %bitcast.4), channel_id=1, source_target_pairs={{8,0},{12,4},{16,8},{20,12},{24,16},{28,20},{0,24},{4,28},{9,1},{1... | collective-permute-start | bytes 1572872 | tf_op jit(solution)/shard_map/ppermute | solution.py:19
  10.7 1.1 collective-permute-start.6
  11.8 0.3 collective-permute-start.5
  12.1 0.2 collective-permute-start.3
  12.3 3.7 %collective-permute-start.2 = (bf16[512,1024]{1,0:T(8,128)(2,1)}, bf16[512,1024]{1,0:T(8,128)(2,1)}, u32[]{:S(2)}, u32[]{:S(2)}) collective-permute-start(bf16[512,1024]{1,0:T(8,128)(2,1)} %bitcast.11), channel_id=1, source_target_pairs={{4,0},{8,4},{12,8},{16,12},{20,16},{24,20},{28,24},{0,28},{5,1},{9... | collective-permute-start | bytes 3145736 | tf_op jit(solution)/shard_map/ppermute | solution.py:19
  16.0 5.6 %collective-permute-done.7.refs_9_ = bf16[256,1024]{1,0:T(8,128)(2,1)S(1)} collective-permute-done((bf16[256,1024]{1,0:T(8,128)(2,1)}, bf16[256,1024]{1,0:T(8,128)(2,1)S(1)}, u32[]{:S(2)}, u32[]{:S(2)}) %collective-permute-start.7) | collective-permute-done | bytes 524320 | tf_op jit(solution)/shard_map/ppermute | solution.py:19
  21.6 1.3 collective-permute-start.1
  22.9 9.9 %collective-permute-done.6.refs_8_ = bf16[256,1024]{1,0:T(8,128)(2,1)S(1)} collective-permute-done((bf16[256,1024]{1,0:T(8,128)(2,1)}, bf16[256,1024]{1,0:T(8,128)(2,1)S(1)}, u32[]{:S(2)}, u32[]{:S(2)}) %collective-permute-start.6) | collective-permute-done | bytes 524320 | tf_op jit(solution)/shard_map/ppermute | solution.py:19
  32.8 0.8 copy-done.1
  33.6 0.0 collective-permute-start
  34.3 0.8 copy.5
  35.1 0.0 collective-permute-done.5.refs_6_
  35.1 1.1 collective-permute-start.4
  36.1 2.1 %fusion.swap = bf16[1024,1024]{1,0:T(8,128)(2,1)} fusion(s32[1024]{0:T(1024)S(1)} %get-tuple-element.5, s32[1024]{0:T(1024)S(1)} %get-tuple-element.8, s32[1024]{0:T(1024)S(1)} %get-tuple-element.6, s32[1024]{0:T(1024)S(1)} %get-tuple-element.7, pred[1024]{0:T(1024)(128)(4,1)S(1)} %get-tuple-element.9, pred[1024]{0:T(1024)(128)(4,1)S(1)} %get-tuple-element.10), kind=kLoop, calls=%fused_computation.1 | loop fusion | flops 6291456 | bytes 2115584 | tf_op jit(solution)/shard_map/convert_element_type | solution.py:26
  38.2 74.2 %collective-permute-done.4.refs_5_ = bf16[256,1024]{1,0:T(8,128)(2,1)S(1)} collective-permute-done((bf16[256,1024]{1,0:T(8,128)(2,1)}, bf16[256,1024]{1,0:T(8,128)(2,1)S(1)}, u32[]{:S(2)}, u32[]{:S(2)}) %collective-permute-start.4) | collective-permute-done | bytes 524320 | tf_op jit(solution)/shard_map/ppermute | solution.py:19
  112.4 0.0 collective-permute-done.3.refs_4_
  112.4 0.0 collective-permute-done.2.refs_3_
  112.4 0.0 collective-permute-done.1.refs_1_
  112.4 0.0 collective-permute-done.refs_0_
  112.4 0.0 copy-done
  112.4 14.0 %shard_map.46 = f32[256,1024]{1,0:T(8,128)} custom-call(s32[1]{0:T(128)S(6)} %copy.6.counts, s32[4,3]{1,0:T(4,128)S(1)} %bitcast.9, bf16[1024,1024]{1,0:T(8,128)(2,1)} %fusion.swap, bf16[512,1024]{1,0:T(8,128)(2,1)S(1)} %collective-permute-done.refs_0_, bf16[512,1024]{1,0:T(8,128)(2,1)S(1)} %collective-permute-done.1.refs_1_, bf16[512,1024]{1,0:T(8,128)(2,1)} %bitcast.14, ...), custom_call_target="tpu_custom_call" | custom-call | tf_op jit(solution)/shard_map/pallas_call | solution.py:101
  126.4 0.0 reduce-scatter.2.cloned.1.call-update
  126.5 53.6 %reduce-scatter.2.cloned.1.call-done = f32[256,256]{1,0:T(8,128)} async-done(((f32[256,1024]{1,0:T(8,128)}), f32[256,256]{1,0:T(8,128)}) %reduce-scatter.2.cloned.1.call-update) | async-done | bytes 262160 | tf_op jit(solution)/shard_map/reduce_scatter | solution.py:132
  (7 shorter events, 0.0 us)
Async XLA Ops:
  6.5 105.9 %copy-start = (bf16[1,256,1024]{2,1,0:T(8,128)(2,1)S(1)}, bf16[1,256,1024]{2,1,0:T(8,128)(2,1)}, u32[]{:S(2)}) copy-start(bf16[1,256,1024]{2,1,0:T(8,128)(2,1)} %param.5) | copy-start | bytes 1572868
  6.5 173.6 %reduce-scatter.2.cloned.1.call-start = ((), (), s32[]{:S(2)}) async-start(), calls=%async_computation.1 | async-start | bytes 1310720 | tf_op jit(solution)/shard_map/reduce_scatter | solution.py:132
  6.5 15.1 %collective-permute-start.7 = (bf16[256,1024]{1,0:T(8,128)(2,1)}, bf16[256,1024]{1,0:T(8,128)(2,1)S(1)}, u32[]{:S(2)}, u32[]{:S(2)}) collective-permute-start(bf16[256,1024]{1,0:T(8,128)(2,1)} %bitcast.4), channel_id=1, source_target_pairs={{8,0},{12,4},{16,8},{20,12},{24,16},{28,20},{0,24},{4,28},{9,1},{1... | collective-permute-start | bytes 1572872 | tf_op jit(solution)/shard_map/ppermute | solution.py:19
  10.7 22.2 %collective-permute-start.6 = (bf16[256,1024]{1,0:T(8,128)(2,1)}, bf16[256,1024]{1,0:T(8,128)(2,1)S(1)}, u32[]{:S(2)}, u32[]{:S(2)}) collective-permute-start(bf16[256,1024]{1,0:T(8,128)(2,1)} %bitcast.5), channel_id=1, source_target_pairs={{4,0},{8,4},{12,8},{16,12},{20,16},{24,20},{28,24},{0,28},{5,1},{9... | collective-permute-start | bytes 1572872 | tf_op jit(solution)/shard_map/ppermute | solution.py:19
  11.8 23.3 %collective-permute-start.5 = (bf16[256,1024]{1,0:T(8,128)(2,1)}, bf16[256,1024]{1,0:T(8,128)(2,1)}, u32[]{:S(2)}, u32[]{:S(2)}) collective-permute-start(bf16[256,1024]{1,0:T(8,128)(2,1)} %bitcast.6), channel_id=1, source_target_pairs={{28,0},{0,4},{4,8},{8,12},{12,16},{16,20},{20,24},{24,28},{29,1},{... | collective-permute-start | bytes 1572872 | tf_op jit(solution)/shard_map/ppermute | solution.py:19
  12.1 100.2 %collective-permute-start.3 = (bf16[512,1024]{1,0:T(8,128)(2,1)}, bf16[512,1024]{1,0:T(8,128)(2,1)}, u32[]{:S(2)}, u32[]{:S(2)}) collective-permute-start(bf16[512,1024]{1,0:T(8,128)(2,1)} %bitcast.10), channel_id=1, source_target_pairs={{8,0},{12,4},{16,8},{20,12},{24,16},{28,20},{0,24},{4,28},{9,1},{1... | collective-permute-start | bytes 3145736 | tf_op jit(solution)/shard_map/ppermute | solution.py:19
  12.3 100.1 %collective-permute-start.2 = (bf16[512,1024]{1,0:T(8,128)(2,1)}, bf16[512,1024]{1,0:T(8,128)(2,1)}, u32[]{:S(2)}, u32[]{:S(2)}) collective-permute-start(bf16[512,1024]{1,0:T(8,128)(2,1)} %bitcast.11), channel_id=1, source_target_pairs={{4,0},{8,4},{12,8},{16,12},{20,16},{24,20},{28,24},{0,28},{5,1},{9... | collective-permute-start | bytes 3145736 | tf_op jit(solution)/shard_map/ppermute | solution.py:19
  21.6 90.8 %collective-permute-start.1 = (bf16[512,1024]{1,0:T(8,128)(2,1)}, bf16[512,1024]{1,0:T(8,128)(2,1)S(1)}, u32[]{:S(2)}, u32[]{:S(2)}) collective-permute-start(bf16[512,1024]{1,0:T(8,128)(2,1)} %bitcast.12), channel_id=1, source_target_pairs={{28,0},{0,4},{4,8},{8,12},{12,16},{16,20},{20,24},{24,28},{29,1},{... | collective-permute-start | bytes 3145736 | tf_op jit(solution)/shard_map/ppermute | solution.py:19
  32.8 0.8 copy-start.1
  33.6 78.8 %collective-permute-start = (bf16[512,1024]{1,0:T(8,128)(2,1)}, bf16[512,1024]{1,0:T(8,128)(2,1)S(1)}, u32[]{:S(2)}, u32[]{:S(2)}) collective-permute-start(bf16[512,1024]{1,0:T(8,128)(2,1)} %bitcast.13), channel_id=1, source_target_pairs={{24,0},{28,4},{0,8},{4,12},{8,16},{12,20},{16,24},{20,28},{25,1},{... | collective-permute-start | bytes 3145736 | tf_op jit(solution)/shard_map/ppermute | solution.py:19
  35.1 77.3 %copy-start.2 = (bf16[256,1024]{1,0:T(8,128)(2,1)S(1)}, bf16[256,1024]{1,0:T(8,128)(2,1)}, u32[]{:S(2)}) copy-start(bf16[256,1024]{1,0:T(8,128)(2,1)} %copy-done.1) | copy-start | bytes 1572868
  35.1 77.3 %collective-permute-start.4 = (bf16[256,1024]{1,0:T(8,128)(2,1)}, bf16[256,1024]{1,0:T(8,128)(2,1)S(1)}, u32[]{:S(2)}, u32[]{:S(2)}) collective-permute-start(bf16[256,1024]{1,0:T(8,128)(2,1)} %bitcast.7), channel_id=1, source_target_pairs={{24,0},{28,4},{0,8},{4,12},{8,16},{12,20},{16,24},{20,28},{25,1},{... | collective-permute-start | bytes 1572872 | tf_op jit(solution)/shard_map/ppermute | solution.py:19
Sparse Core Ops, SparseCore 0:
  126.6 53.4 reduce-scatter.1
where the time goes:
time: 187 us
  waiting for transfers between devices  143 us (76%)
  between operations  14.1 us (8%)
  Pallas kernels  14 us (7%)
  starting transfers between devices  11.8 us (6%)
  other arithmetic  2.09 us (1%)
    ppermute x8, waiting for transfers between devices, shifted(): return lax.ppermute(block, axis, route)  89.7 us
    reduce_scatter x1, waiting for transfers between devices, shards(): lax.psum_scatter(partial_sum, 'aux', scatter_dimension=1, tiled=True)  53.6 us
    pallas_call x1, Pallas kernels, run_tasks(): pl.pallas_call(kernel, out_shape=jax.ShapeDtypeStruct((occ, pairs), jnp.f...  14 us
    ppermute x8, starting transfers between devices, shifted(): return lax.ppermute(block, axis, route)  11.8 us
  transfers between devices with their start and end apart: 9, of which 4 were waited for; matrix products, arithmetic and copies ran while one was open for 2% of the time, Pallas kernels for 0%

commit v1 on v0

v1 whole, which is shorter than its diff:
```python
import functools

import jax
import jax.numpy as jnp
from jax import lax
from jax.experimental import pallas as pl
from jax.experimental.pallas import tpu as pltpu
from jax.sharding import PartitionSpec as P

VB = 32
RADIUS = 2
SPAN = 2 * RADIUS + 1
MOST = 4
LANES = 128
SPREAD = LANES // VB
STEP = 2
N_AUX = 4
MESH = pl.DeviceIdType.MESH


def roll_groups(x, amount):
    if amount == 0:
        return x
    parts = [
        pltpu.roll(x[:, j * LANES : (j + 1) * LANES], amount, 1)
        for j in range(x.shape[1] // LANES)
    ]
    return jnp.concatenate(parts, axis=1)


def cut_rows(depth):
    groups = []
    blocks = depth // LANES
    for b in range(blocks):
        lo = b * LANES
        if b == blocks - 1:
            half = LANES // 2
            groups.append([(lo, half), (lo + half, half)])
        else:
            groups.append([(lo, LANES)])
    return groups


def kernel(
    n_task,
    relayed,
    counts,
    plan,
    fac_in,
    amp_in,
    out,
    fac,
    amp,
    ampt,
    lt,
    right,
    tile,
    swap,
    part,
    inbox,
    xsend,
    xin,
    local_sem,
    fsend,
    frecv,
    tsend,
    trecv,
    qsend,
    qrecv,
    csend,
    crecv,
):
    depth, pairs = fac_in.shape
    occ = amp_in.shape[0]
    share = occ // N_AUX
    blocks = pairs // LANES
    width = pairs // N_AUX
    lanes = STEP * LANES
    t = lax.axis_index("task")
    k = lax.axis_index("aux")
    mate = t + 1 - 2 * (t % 2)
    odd = t % 2

    def aux_peer(bits):
        flip_low = bits % 2
        flip_high = bits // 2
        low = k % 2
        high = k // 2
        if flip_low:
            low = 1 - low
        if flip_high:
            high = 1 - high
        return high * 2 + low

    def wrapped(d):
        return lax.rem(t + d + n_task, n_task)

    if relayed:
        paths = [(wrapped(2), 0), (wrapped(-2), 4), (mate, 1 + 2 * odd)]
        early = [0, 4]
        direct = 3 - 2 * odd
        late = 1 + 2 * odd
        relay_from = 4 - 4 * odd
        relay_to = 3 - 2 * odd
    else:
        paths = [(wrapped(2), 0), (wrapped(-2), 4), (wrapped(1), 1), (wrapped(-1), 3)]
        early = [0, 4]
        direct = 1
        late = 3

    barrier = pltpu.get_barrier_semaphore()
    for peer, _ in paths:
        pl.semaphore_signal(barrier, inc=1, device_id={"task": peer}, device_id_type=MESH)
    for bits in range(1, N_AUX):
        pl.semaphore_signal(
            barrier, inc=1, device_id={"aux": aux_peer(bits)}, device_id_type=MESH
        )
    own_f = pltpu.make_async_copy(fac_in, fac.at[RADIUS], local_sem.at[0])
    own_t = pltpu.make_async_copy(amp_in, amp.at[RADIUS], local_sem.at[1])
    own_f.start()
    own_t.start()
    pl.semaphore_wait(barrier, len(paths) + N_AUX - 1)

    groups = cut_rows(depth)
    pieces = [piece for group in groups for piece in group]
    mine = pl.ds(pl.multiple_of(k * share, share), share)

    def send_piece(i, path, peer, src, slot):
        lo, size = pieces[i]
        return pltpu.make_async_remote_copy(
            src_ref=src.at[pl.ds(lo, size)],
            dst_ref=fac.at[slot, pl.ds(lo, size)],
            send_sem=fsend.at[path, i],
            recv_sem=frecv.at[slot, i],
            device_id={"task": peer},
            device_id_type=MESH,
        )

    def send_amp(path, peer, src, slot):
        return pltpu.make_async_remote_copy(
            src_ref=src,
            dst_ref=amp.at[slot, mine],
            send_sem=tsend.at[path],
            recv_sem=trecv.at[slot],
            device_id={"task": peer},
            device_id_type=MESH,
        )

    def spread_amp(slot, order, bits):
        return pltpu.make_async_remote_copy(
            src_ref=amp.at[slot, mine],
            dst_ref=amp.at[slot, mine],
            send_sem=qsend.at[order, bits - 1],
            recv_sem=qrecv.at[slot, bits - 1],
            device_id={"aux": aux_peer(bits)},
            device_id_type=MESH,
        )

    started = []

    def start(copy):
        copy.start()
        started.append(copy)

    for path, (peer, slot) in enumerate(paths):
        start(send_amp(path, peer, amp_in.at[mine], slot))
    for i in range(len(pieces)):
        for path, (peer, slot) in enumerate(paths):
            start(send_piece(i, path, peer, fac_in, slot))

    @pl.loop(0, blocks)
    def _(j):
        base = pl.multiple_of(j * LANES, LANES)
        rows = lax.broadcasted_iota(jnp.int32, (LANES, pairs), 0) + base
        cols = lax.broadcasted_iota(jnp.int32, (LANES, pairs), 1)
        hit = rows == (cols % VB) * VB + cols // VB
        swap[pl.ds(base, LANES), :] = hit.astype(jnp.float32).astype(jnp.bfloat16)

    def prepare(slot, b):
        span = pl.ds(b * LANES, LANES)
        x = fac[slot, span, :]
        for hi in range(blocks):
            strip = x[:, hi * LANES : (hi + 1) * LANES].T
            for s in range(SPREAD):
                lt[slot, s, hi * VB : (hi + 1) * VB, span] = strip[s * VB : (s + 1) * VB, :]
        swapped = jnp.dot(x, swap[...], preferred_element_type=jnp.float32)
        for s in range(SPREAD):
            right[slot, s, span, :] = roll_groups(swapped, s * VB).astype(jnp.bfloat16)

    def prepare_amp(slot):
        ampt[slot] = jnp.dot(
            amp[slot], swap[...], preferred_element_type=jnp.float32
        ).astype(jnp.bfloat16)

    def amp_arrived(slot, order):
        send_amp(0, t, amp_in.at[mine], slot).wait_recv()
        for bits in range(1, N_AUX):
            start(spread_amp(slot, order, bits))

    def amp_ready(slot, order):
        for bits in range(1, N_AUX):
            spread_amp(slot, order, bits).wait_recv()
        prepare_amp(slot)

    def arrived(slot, i):
        send_piece(i, 0, t, fac_in, slot).wait_recv()

    own_t.wait()
    own_f.wait()
    prepare_amp(RADIUS)
    for b in range(len(groups)):
        prepare(RADIUS, b)

    for order, slot in enumerate(early):
        amp_arrived(slot, order)
    if relayed:
        start(send_amp(3, mate, amp.at[relay_from, mine], relay_to))
    amp_arrived(direct, 2)

    first = 0
    for b, group in enumerate(groups):
        for i in range(first, first + len(group)):
            for slot in early:
                arrived(slot, i)
            if relayed:
                start(send_piece(i, 3, mate, fac.at[relay_from], relay_to))
        if b > 0:
            previous = len(groups[b - 1])
            for i in range(first - previous, first):
                arrived(late, i)
            prepare(late, b - 1)
        for i in range(first, first + len(group)):
            arrived(direct, i)
        for slot in early + [direct]:
            prepare(slot, b)
        if b == 0:
            amp_arrived(late, 3)
            for order, slot in enumerate(early):
                amp_ready(slot, order)
        if b == 1:
            amp_ready(direct, 2)
            amp_ready(late, 3)
        first += len(group)
    for i in range(first - len(groups[-1]), first):
        arrived(late, i)
    prepare(late, len(groups) - 1)

    half_rows = blocks * VB
    group_of = (lax.broadcasted_iota(jnp.int32, (half_rows, lanes), 1) // VB) % SPREAD

    @pl.loop(0, MOST)
    def _(slot):
        left_tile, right_tile = plan[0, 0, slot], plan[1, 0, slot]

        @pl.loop(0, blocks // STEP)
        def _(step):
            base = pl.multiple_of(step * lanes, lanes)
            outs = [
                jnp.dot(
                    lt[left_tile, s],
                    right[right_tile, s, :, pl.ds(base, lanes)],
                    preferred_element_type=jnp.float32,
                )
                for s in range(SPREAD)
            ]
            for d in range(SPREAD):
                mixed = outs[(SPREAD - 1 - d) % SPREAD]
                for g in range(SPREAD - 1):
                    mixed = jnp.where(group_of == g, outs[(g - d) % SPREAD], mixed)
                mixed = roll_groups(mixed, (LANES - d * VB) % LANES).astype(jnp.bfloat16)
                for j in range(STEP):
                    row = pl.multiple_of(base + (j * SPREAD + d) * VB, VB)
                    for hi in range(blocks):
                        tile[slot, pl.ds(row, VB), hi * LANES : (hi + 1) * LANES] = mixed[
                            hi * VB : (hi + 1) * VB, j * LANES : (j + 1) * LANES
                        ]

    low = k % 2
    high = k // 2

    def swap_sums(stage, bits, src, dst):
        return pltpu.make_async_remote_copy(
            src_ref=src,
            dst_ref=dst,
            send_sem=csend.at[stage],
            recv_sem=crecv.at[stage],
            device_id={"aux": aux_peer(bits)},
            device_id_type=MESH,
        )

    for stage, side in enumerate((1 - high, high)):
        cols = pl.ds(pl.multiple_of(side * 2 * width, 2 * width), 2 * width)
        total = jnp.zeros((occ, 2 * width), jnp.float32)
        for slot in range(MOST):
            term = jnp.dot(
                ampt[plan[2, 0, slot]], tile[slot, :, cols], preferred_element_type=jnp.float32
            )
            total += jnp.where(slot < counts[0], term, 0.0)
        part[stage, 0] = total[:, :width]
        part[stage, 1] = total[:, width:]
        pair = swap_sums(stage, 1, part.at[stage, 1 - low], inbox.at[stage])
        start(pair)
        if stage == 0:
            pair.wait_recv()
            xsend[...] = part[stage, low] + inbox[stage]
            far = swap_sums(2, 2, xsend, xin)
            start(far)
        else:
            pair.wait_recv()
            far.wait_recv()
            out[...] = part[stage, low] + inbox[stage] + xin[...]

    for copy in started:
        copy.wait_send()


def run(factors, amplitudes, counts, plan, n_task, relayed):
    depth, pairs = factors.shape
    occ = amplitudes.shape[0]
    width = pairs // N_AUX
    n_pieces = sum(len(group) for group in cut_rows(depth))
    anywhere = pl.BlockSpec(memory_space=pl.ANY)
    scalars = pl.BlockSpec(memory_space=pltpu.SMEM)
    dma = pltpu.SemaphoreType.DMA
    return pl.pallas_call(
        functools.partial(kernel, n_task, relayed),
        out_shape=jax.ShapeDtypeStruct((occ, width), jnp.float32),
        in_specs=[scalars, scalars, anywhere, anywhere],
        out_specs=pl.BlockSpec(memory_space=pltpu.VMEM),
        scratch_shapes=[
            pltpu.VMEM((SPAN, depth, pairs), jnp.bfloat16),
            pltpu.VMEM((SPAN, occ, pairs), jnp.bfloat16),
            pltpu.VMEM((SPAN, occ, pairs), jnp.bfloat16),
            pltpu.VMEM((SPAN, SPREAD, pairs // SPREAD, depth), jnp.bfloat16),
            pltpu.VMEM((SPAN, SPREAD, depth, pairs), jnp.bfloat16),
            pltpu.VMEM((MOST, pairs, pairs), jnp.bfloat16),
            pltpu.VMEM((pairs, pairs), jnp.bfloat16),
            pltpu.VMEM((2, 2, occ, width), jnp.float32),
            pltpu.VMEM((2, occ, width), jnp.float32),
            pltpu.VMEM((occ, width), jnp.float32),
            pltpu.VMEM((occ, width), jnp.float32),
            dma((2,)),
            dma((4, n_pieces)),
            dma((SPAN, n_pieces)),
            dma((4,)),
            dma((SPAN,)),
            dma((4, N_AUX - 1)),
            dma((SPAN, N_AUX - 1)),
            dma((3,)),
            dma((3,)),
        ],
        compiler_params=pltpu.CompilerParams(
            vmem_limit_bytes=60 * 1024 * 1024, collective_id=0, has_side_effects=True
        ),
    )(counts, plan, factors, amplitudes)


def solution(mesh):
    n_task, n_aux = mesh.shape["task"], mesh.shape["aux"]
    assert n_aux == N_AUX
    relayed = n_task == 8

    def shards(factors, amplitudes, task_counts, task_tiles):
        plan = jnp.transpose(task_tiles, (2, 0, 1))
        total = run(factors[0], amplitudes[0], task_counts, plan, n_task, relayed)
        return total[None]

    return jax.shard_map(
        shards,
        mesh=mesh,
        in_specs=(P("task", "aux", None), P("task", None, None), P("task"), P("task", None, None)),
        out_specs=P("task", None, "aux"),
        check_vma=False,
    )
```

time: 187 us -> 85.7 us (0.46)
  waiting for transfers between devices: 143 us -> 0 us
  Pallas kernels: 14 us -> 83.2 us
  between operations: 14.1 us -> 0.66 us
  starting transfers between devices: 11.8 us -> 0 us
  other arithmetic: 2.09 us -> 0 us
    ppermute x8 -> x0, waiting for transfers between devices: 89.7 us -> none  [shifted(): return lax.ppermute(block, axis, route)]
    pallas_call x1, Pallas kernels: 14 us -> 83.2 us  [run(): pl.pallas_call(functools.partial(kernel, n_task, relayed), out_shape=jax....]
    reduce_scatter x1 -> x0, waiting for transfers between devices: 53.6 us -> none  [shards(): lax.psum_scatter(partial_sum, 'aux', scatter_dimension=1, tiled=True)]
    ppermute x8 -> x0, starting transfers between devices: 11.8 us -> none  [shifted(): return lax.ppermute(block, axis, route)]
    convert_element_type x1 -> x0, other arithmetic: 2.07 us -> none  [swap_matrix(): return (rows == cols % width * width + cols // width).astype(jnp.bfloat16)]
  transfers between devices with their start and end apart: 9 -> 0, of which waited for: 4 -> 0; matrix products, arithmetic and copies ran while one was open for 2% -> 0% of each run, Pallas kernels for 0% -> 0%
where the time goes in v1:
time: 85.7 us; the launch traced here: 85.5 us
  Pallas kernels  83.2 us (97%)
  local copies, waits for them, and re-layouts  1.67 us (2%)
    pallas_call x1, Pallas kernels, run(): pl.pallas_call(functools.partial(kernel, n_task, relayed), out_shape=jax....  83.2 us

profile of v1, /device:TPU:1, one launch (start us, length us, event | category | flops | bytes accessed | tf_op | source)
XLA Modules:
  0.0 85.5 jit_solution(3450623985881294488)
XLA Ops:
  0.7 83.2 %shard_map.46 = f32[256,256]{1,0:T(8,128)} custom-call(s32[1]{0:T(128)S(6)} %copy.6.counts, s32[3,1,4]{2,1,0:T(1,128)} %bitcast.7, bf16[512,1024]{1,0:T(8,128)(2,1)} %bitcast.4, bf16[256,1024]{1,0:T(8,128)(2,1)} %bitcast.6), custom_call_target="tpu_custom_call" | custom-call | tf_op jit(solution)/shard_map/pallas_call | solution.py:325
  83.9 1.7 %copy.7 = f32[1,256,256]{2,1,0:T(8,128)} copy(f32[1,256,256]{2,1,0:T(8,128)} %bitcast.5) | data formatting | bytes 524288

commit v2 on v1

--- a/solution.py
+++ b/solution.py
@@ -15,6 +15,7 @@
 SPREAD = LANES // VB
 STEP = 2
 N_AUX = 4
+TRIGGER = 2
 MESH = pl.DeviceIdType.MESH
 
 
@@ -54,7 +55,7 @@
     ampt,
     lt,
     right,
-    tile,
+    vacc,
     swap,
     part,
     inbox,
@@ -96,17 +97,16 @@
         return lax.rem(t + d + n_task, n_task)
 
     if relayed:
-        paths = [(wrapped(2), 0), (wrapped(-2), 4), (mate, 1 + 2 * odd)]
-        early = [0, 4]
-        direct = 3 - 2 * odd
-        late = 1 + 2 * odd
-        relay_from = 4 - 4 * odd
+        paths = [
+            (wrapped(4 * odd - 2), 4 - 4 * odd),
+            (mate, 1 + 2 * odd),
+            (wrapped(2 - 4 * odd), 4 * odd),
+        ]
+        ahead, near, behind, late = 4 - 4 * odd, 3 - 2 * odd, 4 * odd, 1 + 2 * odd
         relay_to = 3 - 2 * odd
     else:
-        paths = [(wrapped(2), 0), (wrapped(-2), 4), (wrapped(1), 1), (wrapped(-1), 3)]
-        early = [0, 4]
-        direct = 1
-        late = 3
+        paths = [(wrapped(2), 0), (wrapped(-1), 3), (wrapped(-2), 4), (wrapped(1), 1)]
+        ahead, near, behind, late = 0, 3, 4, 1
 
     barrier = pltpu.get_barrier_semaphore()
     for peer, _ in paths:
@@ -123,6 +123,7 @@
 
     groups = cut_rows(depth)
     pieces = [piece for group in groups for piece in group]
+    held = depth // 2
     mine = pl.ds(pl.multiple_of(k * share, share), share)
 
     def send_piece(i, path, peer, src, slot):
@@ -162,11 +163,18 @@
         copy.start()
         started.append(copy)
 
+    def send_own(path):
+        peer, slot = paths[path]
+        for i in range(len(pieces)):
+            start(send_piece(i, path, peer, fac_in, slot))
+
     for path, (peer, slot) in enumerate(paths):
         start(send_amp(path, peer, amp_in.at[mine], slot))
-    for i in range(len(pieces)):
-        for path, (peer, slot) in enumerate(paths):
-            start(send_piece(i, path, peer, fac_in, slot))
+    send_own(0)
+    send_own(1)
+    if not relayed:
+        send_own(2)
+        send_own(3)
 
     @pl.loop(0, blocks)
     def _(j):
@@ -177,15 +185,18 @@
         swap[pl.ds(base, LANES), :] = hit.astype(jnp.float32).astype(jnp.bfloat16)
 
     def prepare(slot, b):
-        span = pl.ds(b * LANES, LANES)
-        x = fac[slot, span, :]
+        x = fac[slot, pl.ds(b * LANES, LANES), :]
+        part_of, lo = b * LANES // held, b * LANES % held
+        span = pl.ds(lo, LANES)
         for hi in range(blocks):
             strip = x[:, hi * LANES : (hi + 1) * LANES].T
             for s in range(SPREAD):
-                lt[slot, s, hi * VB : (hi + 1) * VB, span] = strip[s * VB : (s + 1) * VB, :]
+                lt[part_of, slot, s, hi * VB : (hi + 1) * VB, span] = strip[
+                    s * VB : (s + 1) * VB, :
+                ]
         swapped = jnp.dot(x, swap[...], preferred_element_type=jnp.float32)
         for s in range(SPREAD):
-            right[slot, s, span, :] = roll_groups(swapped, s * VB).astype(jnp.bfloat16)
+            right[part_of, slot, s, span, :] = roll_groups(swapped, s * VB).astype(jnp.bfloat16)
 
     def prepare_amp(slot):
         ampt[slot] = jnp.dot(
@@ -197,9 +208,9 @@
         for bits in range(1, N_AUX):
             start(spread_amp(slot, order, bits))
 
-    def amp_ready(slot, order):
+    def amp_ready(slot):
         for bits in range(1, N_AUX):
-            spread_amp(slot, order, bits).wait_recv()
+            spread_amp(slot, 0, bits).wait_recv()
         prepare_amp(slot)
 
     def arrived(slot, i):
@@ -211,69 +222,87 @@
     for b in range(len(groups)):
         prepare(RADIUS, b)
 
-    for order, slot in enumerate(early):
-        amp_arrived(slot, order)
+    amp_arrived(ahead, 0)
     if relayed:
-        start(send_amp(3, mate, amp.at[relay_from, mine], relay_to))
-    amp_arrived(direct, 2)
-
-    first = 0
+        start(send_amp(3, mate, amp.at[ahead, mine], relay_to))
+    amp_arrived(near, 1)
+    amp_arrived(behind, 2)
+
+    i = 0
     for b, group in enumerate(groups):
-        for i in range(first, first + len(group)):
-            for slot in early:
-                arrived(slot, i)
+        for _ in group:
+            arrived(ahead, i)
             if relayed:
-                start(send_piece(i, 3, mate, fac.at[relay_from], relay_to))
-        if b > 0:
-            previous = len(groups[b - 1])
-            for i in range(first - previous, first):
-                arrived(late, i)
-            prepare(late, b - 1)
-        for i in range(first, first + len(group)):
-            arrived(direct, i)
-        for slot in early + [direct]:
-            prepare(slot, b)
+                start(send_piece(i, 3, mate, fac.at[ahead], relay_to))
+                if i == len(pieces) - TRIGGER:
+                    send_own(2)
+            i += 1
+        prepare(ahead, b)
+        for j in range(i - len(group), i):
+            arrived(near, j)
+        prepare(near, b)
         if b == 0:
             amp_arrived(late, 3)
-            for order, slot in enumerate(early):
-                amp_ready(slot, order)
         if b == 1:
-            amp_ready(direct, 2)
-            amp_ready(late, 3)
-        first += len(group)
-    for i in range(first - len(groups[-1]), first):
-        arrived(late, i)
-    prepare(late, len(groups) - 1)
-
-    half_rows = blocks * VB
-    group_of = (lax.broadcasted_iota(jnp.int32, (half_rows, lanes), 1) // VB) % SPREAD
+            for slot in (ahead, near, behind, late):
+                amp_ready(slot)
+
+    lane_blocks = blocks // STEP
+
+    def product(part_of, slot, s, cols):
+        return jnp.dot(
+            lt[part_of, plan[0, 0, slot], s],
+            right[part_of, plan[1, 0, slot], s, :, cols],
+            preferred_element_type=jnp.float32,
+        )
+
+    i = 0
+    for b, group in enumerate(groups):
+        for slot in (behind, late):
+            for j in range(i, i + len(group)):
+                arrived(slot, j)
+            prepare(slot, b)
+        i += len(group)
+        if (b + 1) * LANES == held:
+
+            @pl.loop(0, MOST)
+            def _(slot):
+                @pl.loop(0, lane_blocks)
+                def _(step):
+                    cols = pl.ds(pl.multiple_of(step * lanes, lanes), lanes)
+                    for s in range(SPREAD):
+                        vacc[slot, s, :, cols] = product(0, slot, s, cols)
+
+    flat = right.at[0]
+    group_of = (lax.broadcasted_iota(jnp.int32, (blocks * VB, LANES), 1) // VB).astype(
+        jnp.float32
+    )
+    is_odd = (group_of == 1.0) | (group_of == 3.0)
+    is_high = group_of >= 2.0
 
     @pl.loop(0, MOST)
     def _(slot):
-        left_tile, right_tile = plan[0, 0, slot], plan[1, 0, slot]
-
-        @pl.loop(0, blocks // STEP)
+        @pl.loop(0, lane_blocks)
         def _(step):
-            base = pl.multiple_of(step * lanes, lanes)
-            outs = [
-                jnp.dot(
-                    lt[left_tile, s],
-                    right[right_tile, s, :, pl.ds(base, lanes)],
-                    preferred_element_type=jnp.float32,
-                )
-                for s in range(SPREAD)
-            ]
+            cols = pl.ds(pl.multiple_of(step * lanes, lanes), lanes)
+            for s in range(SPREAD):
+                whole = vacc[slot, s, :, cols] + product(1, slot, s, cols)
+                flat[MOST, s, :, cols] = whole.astype(jnp.bfloat16)
+
+        for db in range(blocks):
+            x = [flat[MOST, s, :, db * LANES : (db + 1) * LANES] for s in range(SPREAD)]
+            p = [jnp.where(is_odd, x[(j + 1) % SPREAD], x[j]) for j in range(SPREAD)]
+            w = [jnp.where(is_high, p[(j + 2) % SPREAD], p[j]) for j in range(SPREAD)]
             for d in range(SPREAD):
-                mixed = outs[(SPREAD - 1 - d) % SPREAD]
-                for g in range(SPREAD - 1):
-                    mixed = jnp.where(group_of == g, outs[(g - d) % SPREAD], mixed)
-                mixed = roll_groups(mixed, (LANES - d * VB) % LANES).astype(jnp.bfloat16)
-                for j in range(STEP):
-                    row = pl.multiple_of(base + (j * SPREAD + d) * VB, VB)
-                    for hi in range(blocks):
-                        tile[slot, pl.ds(row, VB), hi * LANES : (hi + 1) * LANES] = mixed[
-                            hi * VB : (hi + 1) * VB, j * LANES : (j + 1) * LANES
-                        ]
+                mixed = roll_groups(w[-d % SPREAD], (LANES - d * VB) % LANES)
+                row = (db * SPREAD + d) * VB
+                for hi in range(blocks):
+                    flat[
+                        slot,
+                        row // (blocks * VB),
+                        pl.ds(row % (blocks * VB), VB),
+                        hi * LANES : (hi + 1) * LANES,
+                    ] = mixed[hi * VB : (hi + 1) * VB, :]
 
     low = k % 2
     high = k // 2
@@ -292,8 +321,9 @@
         cols = pl.ds(pl.multiple_of(side * 2 * width, 2 * width), 2 * width)
         total = jnp.zeros((occ, 2 * width), jnp.float32)
         for slot in range(MOST):
+            weights = flat[slot, :, :, cols].reshape(pairs, 2 * width)
             term = jnp.dot(
-                ampt[plan[2, 0, slot]], tile[slot, :, cols], preferred_element_type=jnp.float32
+                ampt[plan[2, 0, slot]], weights, preferred_element_type=jnp.float32
             )
             total += jnp.where(slot < counts[0], term, 0.0)
         part[stage, 0] = total[:, :width]
@@ -302,13 +332,13 @@
         start(pair)
         if stage == 0:
             pair.wait_recv()
-            xsend[...] = part[stage, low] + inbox[stage]
+            xsend[...] = (part[stage, low] + inbox[stage]).astype(xsend.dtype)
             far = swap_sums(2, 2, xsend, xin)
             start(far)
         else:
             pair.wait_recv()
             far.wait_recv()
-            out[...] = part[stage, low] + inbox[stage] + xin[...]
+            out[...] = part[stage, low] + inbox[stage] + xin[...].astype(jnp.float32)
 
     for copy in started:
         copy.wait_send()
@@ -331,9 +361,9 @@
             pltpu.VMEM((SPAN, depth, pairs), jnp.bfloat16),
             pltpu.VMEM((SPAN, occ, pairs), jnp.bfloat16),
             pltpu.VMEM((SPAN, occ, pairs), jnp.bfloat16),
-            pltpu.VMEM((SPAN, SPREAD, pairs // SPREAD, depth), jnp.bfloat16),
-            pltpu.VMEM((SPAN, SPREAD, depth, pairs), jnp.bfloat16),
-            pltpu.VMEM((MOST, pairs, pairs), jnp.bfloat16),
+            pltpu.VMEM((2, SPAN, SPREAD, pairs // SPREAD, depth // 2), jnp.bfloat16),
+            pltpu.VMEM((2, SPAN, SPREAD, depth // 2, pairs), jnp.bfloat16),
+            pltpu.VMEM((MOST, SPREAD, pairs // SPREAD, pairs), jnp.float32),
             pltpu.VMEM((pairs, pairs), jnp.bfloat16),
             pltpu.VMEM((2, 2, occ, width), jnp.float32),
             pltpu.VMEM((2, occ, width), jnp.float32),

time: 85.7 us -> 105 us (1.23); the launches traced: 85.5 us -> 103 us
  Pallas kernels: 83.2 us -> 101 us
    pallas_call x1, Pallas kernels: 83.2 us -> 101 us  [run(): pl.pallas_call(functools.partial(kernel, n_task, relayed), out_shape=jax....]
where the time goes in v2:
time: 105 us; the launch traced here: 103 us
  Pallas kernels  101 us (96%)
  local copies, waits for them, and re-layouts  1.67 us (2%)
    pallas_call x1, Pallas kernels, run(): pl.pallas_call(functools.partial(kernel, n_task, relayed), out_shape=jax....  101 us

profile of v2, /device:TPU:1, one launch (start us, length us, event | category | flops | bytes accessed | tf_op | source)
XLA Modules:
  0.0 103.5 jit_solution(9584369705028312651)
XLA Ops:
  0.7 101.1 %shard_map.46 = f32[256,256]{1,0:T(8,128)} custom-call(s32[1]{0:T(128)S(6)} %copy.6.counts, s32[3,1,4]{2,1,0:T(1,128)} %bitcast.7, bf16[512,1024]{1,0:T(8,128)(2,1)} %bitcast.4, bf16[256,1024]{1,0:T(8,128)(2,1)} %bitcast.6), custom_call_target="tpu_custom_call" | custom-call | tf_op jit(solution)/shard_map/pallas_call | solution.py:355
  101.8 1.7 %copy.7 = f32[1,256,256]{2,1,0:T(8,128)} copy(f32[1,256,256]{2,1,0:T(8,128)} %bitcast.5) | data formatting | bytes 524288

commit v3 on v2

--- a/solution.py
+++ b/solution.py
@@ -15,7 +15,6 @@
 SPREAD = LANES // VB
 STEP = 2
 N_AUX = 4
-TRIGGER = 2
 MESH = pl.DeviceIdType.MESH
 
 
@@ -42,7 +41,24 @@
     return groups
 
 
-def kernel(
+def kernel(n_task, relayed, counts, plan, fac_in, amp_in, out, *scratch):
+    depth, pairs = fac_in.shape
+    occ = amp_in.shape[0]
+    rows = pairs // SPREAD
+    body = functools.partial(
+        scoped_kernel, n_task, relayed, counts, plan, fac_in, amp_in, out, *scratch
+    )
+    pl.run_scoped(
+        body,
+        ampt=pltpu.VMEM((SPAN, occ, pairs), jnp.bfloat16),
+        lt=pltpu.VMEM((2, SPAN, SPREAD, rows, depth // 2), jnp.bfloat16),
+        right=pltpu.VMEM((2, SPAN, SPREAD, depth // 2, pairs), jnp.bfloat16),
+        vacc=pltpu.VMEM((MOST, SPREAD, rows, pairs), jnp.float32),
+        swap=pltpu.VMEM((pairs, pairs), jnp.bfloat16),
+    )
+
+
+def scoped_kernel(
     n_task,
     relayed,
     counts,
@@ -52,11 +68,6 @@
     out,
     fac,
     amp,
-    ampt,
-    lt,
-    right,
-    vacc,
-    swap,
     part,
     inbox,
     xsend,
@@ -70,6 +81,11 @@
     qrecv,
     csend,
     crecv,
+    ampt,
+    lt,
+    right,
+    vacc,
+    swap,
 ):
     depth, pairs = fac_in.shape
     occ = amp_in.shape[0]
@@ -172,8 +188,8 @@
         start(send_amp(path, peer, amp_in.at[mine], slot))
     send_own(0)
     send_own(1)
+    send_own(2)
     if not relayed:
-        send_own(2)
         send_own(3)
 
     @pl.loop(0, blocks)
@@ -234,8 +250,6 @@
             arrived(ahead, i)
             if relayed:
                 start(send_piece(i, 3, mate, fac.at[ahead], relay_to))
-                if i == len(pieces) - TRIGGER:
-                    send_own(2)
             i += 1
         prepare(ahead, b)
         for j in range(i - len(group), i):
@@ -273,36 +287,34 @@
                     for s in range(SPREAD):
                         vacc[slot, s, :, cols] = product(0, slot, s, cols)
 
-    flat = right.at[0]
-    group_of = (lax.broadcasted_iota(jnp.int32, (blocks * VB, LANES), 1) // VB).astype(
-        jnp.float32
-    )
-    is_odd = (group_of == 1.0) | (group_of == 3.0)
-    is_high = group_of >= 2.0
+    tile = right.at[0]
+    height = blocks * VB
+    group_of = lax.broadcasted_iota(jnp.int32, (height, LANES), 1) // VB
+    is_odd = (group_of % 2).astype(jnp.float32).astype(jnp.bfloat16) > 0.5
+    is_high = group_of.astype(jnp.float32).astype(jnp.bfloat16) > 1.5
 
     @pl.loop(0, MOST)
     def _(slot):
-        @pl.loop(0, lane_blocks)
-        def _(step):
-            cols = pl.ds(pl.multiple_of(step * lanes, lanes), lanes)
+        for step in range(lane_blocks):
+            outs = []
             for s in range(SPREAD):
+                cols = pl.ds(step * lanes, lanes)
                 whole = vacc[slot, s, :, cols] + product(1, slot, s, cols)
-                flat[MOST, s, :, cols] = whole.astype(jnp.bfloat16)
-
-        for db in range(blocks):
-            x = [flat[MOST, s, :, db * LANES : (db + 1) * LANES] for s in range(SPREAD)]
-            p = [jnp.where(is_odd, x[(j + 1) % SPREAD], x[j]) for j in range(SPREAD)]
-            w = [jnp.where(is_high, p[(j + 2) % SPREAD], p[j]) for j in range(SPREAD)]
-            for d in range(SPREAD):
-                mixed = roll_groups(w[-d % SPREAD], (LANES - d * VB) % LANES)
-                row = (db * SPREAD + d) * VB
-                for hi in range(blocks):
-                    flat[
-                        slot,
-                        row // (blocks * VB),
-                        pl.ds(row % (blocks * VB), VB),
-                        hi * LANES : (hi + 1) * LANES,
-                    ] = mixed[hi * VB : (hi + 1) * VB, :]
+                outs.append(whole.astype(jnp.bfloat16))
+            for j in range(STEP):
+                x = [o[:, j * LANES : (j + 1) * LANES] for o in outs]
+                p = [jnp.where(is_odd, x[(n + 1) % SPREAD], x[n]) for n in range(SPREAD)]
+                w = [jnp.where(is_high, p[(n + 2) % SPREAD], p[n]) for n in range(SPREAD)]
+                for d in range(SPREAD):
+                    mixed = w[-d % SPREAD]
+                    if d > 0:
+                        mixed = pltpu.roll(mixed, LANES - d * VB, 1)
+                    row = ((step * STEP + j) * SPREAD + d) * VB
+                    at = pl.ds(row % height, VB)
+                    for hi in range(blocks):
+                        tile[slot, row // height, at, hi * LANES : (hi + 1) * LANES] = mixed[
+                            hi * VB : (hi + 1) * VB, :
+                        ]
 
     low = k % 2
     high = k // 2
@@ -321,7 +333,7 @@
         cols = pl.ds(pl.multiple_of(side * 2 * width, 2 * width), 2 * width)
         total = jnp.zeros((occ, 2 * width), jnp.float32)
         for slot in range(MOST):
-            weights = flat[slot, :, :, cols].reshape(pairs, 2 * width)
+            weights = tile[slot, :, :, cols].reshape(pairs, 2 * width)
             term = jnp.dot(
                 ampt[plan[2, 0, slot]], weights, preferred_element_type=jnp.float32
             )
@@ -360,11 +372,6 @@
         scratch_shapes=[
             pltpu.VMEM((SPAN, depth, pairs), jnp.bfloat16),
             pltpu.VMEM((SPAN, occ, pairs), jnp.bfloat16),
-            pltpu.VMEM((SPAN, occ, pairs), jnp.bfloat16),
-            pltpu.VMEM((2, SPAN, SPREAD, pairs // SPREAD, depth // 2), jnp.bfloat16),
-            pltpu.VMEM((2, SPAN, SPREAD, depth // 2, pairs), jnp.bfloat16),
-            pltpu.VMEM((MOST, SPREAD, pairs // SPREAD, pairs), jnp.float32),
-            pltpu.VMEM((pairs, pairs), jnp.bfloat16),
             pltpu.VMEM((2, 2, occ, width), jnp.float32),
             pltpu.VMEM((2, occ, width), jnp.float32),
             pltpu.VMEM((occ, width), jnp.float32),

time: 105 us -> 79.8 us (0.76); the launches traced: 103 us -> 79.6 us
  Pallas kernels: 101 us -> 77.3 us
    pallas_call x1, Pallas kernels: 101 us -> 77.3 us  [run(): pl.pallas_call(functools.partial(kernel, n_task, relayed), out_shape=jax....]
where the time goes in v3:
time: 79.8 us; the launch traced here: 79.6 us
  Pallas kernels  77.3 us (97%)
  local copies, waits for them, and re-layouts  1.67 us (2%)
    pallas_call x1, Pallas kernels, run(): pl.pallas_call(functools.partial(kernel, n_task, relayed), out_shape=jax....  77.3 us
    unnamed x1, local copies, waits for them, and re-layouts  1.67 us

profile of v3, /device:TPU:1, one launch (start us, length us, event | category | flops | bytes accessed | tf_op | source)
XLA Modules:
  0.0 79.6 jit_solution(10542751635235469342)
XLA Ops:
  0.7 77.3 %shard_map.46 = f32[256,256]{1,0:T(8,128)} custom-call(s32[1]{0:T(128)S(6)} %copy.6.counts, s32[3,1,4]{2,1,0:T(1,128)} %bitcast.7, bf16[512,1024]{1,0:T(8,128)(2,1)} %bitcast.4, bf16[256,1024]{1,0:T(8,128)(2,1)} %bitcast.6), custom_call_target="tpu_custom_call" | custom-call | tf_op jit(solution)/shard_map/pallas_call | solution.py:367
  78.0 1.7 %copy.7 = f32[1,256,256]{2,1,0:T(8,128)} copy(f32[1,256,256]{2,1,0:T(8,128)} %bitcast.5) | data formatting | bytes 524288

commit v4 on v3

--- a/solution.py
+++ b/solution.py
@@ -15,6 +15,7 @@
 SPREAD = LANES // VB
 STEP = 2
 N_AUX = 4
+PAIR = 2
 MESH = pl.DeviceIdType.MESH
 
 
@@ -41,18 +42,18 @@
     return groups
 
 
-def kernel(n_task, relayed, counts, plan, fac_in, amp_in, out, *scratch):
+def kernel(n_task, relayed, counts_in, plan_in, fac_in, amp_in, out, *scratch):
     depth, pairs = fac_in.shape
     occ = amp_in.shape[0]
     rows = pairs // SPREAD
     body = functools.partial(
-        scoped_kernel, n_task, relayed, counts, plan, fac_in, amp_in, out, *scratch
+        scoped_kernel, n_task, relayed, counts_in, plan_in, fac_in, amp_in, out, *scratch
     )
     pl.run_scoped(
         body,
         ampt=pltpu.VMEM((SPAN, occ, pairs), jnp.bfloat16),
         lt=pltpu.VMEM((2, SPAN, SPREAD, rows, depth // 2), jnp.bfloat16),
-        right=pltpu.VMEM((2, SPAN, SPREAD, depth // 2, pairs), jnp.bfloat16),
+        right_a=pltpu.VMEM((SPAN, SPREAD, depth // 2, pairs), jnp.bfloat16),
         vacc=pltpu.VMEM((MOST, SPREAD, rows, pairs), jnp.float32),
         swap=pltpu.VMEM((pairs, pairs), jnp.bfloat16),
     )
@@ -61,17 +62,20 @@
 def scoped_kernel(
     n_task,
     relayed,
-    counts,
-    plan,
+    counts_in,
+    plan_in,
     fac_in,
     amp_in,
     out,
     fac,
     amp,
+    right_b,
     part,
     inbox,
     xsend,
     xin,
+    counts,
+    plan,
     local_sem,
     fsend,
     frecv,
@@ -83,7 +87,7 @@
     crecv,
     ampt,
     lt,
-    right,
+    right_a,
     vacc,
     swap,
 ):
@@ -133,13 +137,16 @@
         )
     own_f = pltpu.make_async_copy(fac_in, fac.at[RADIUS], local_sem.at[0])
     own_t = pltpu.make_async_copy(amp_in, amp.at[RADIUS], local_sem.at[1])
-    own_f.start()
-    own_t.start()
+    own_c = pltpu.make_async_copy(counts_in, counts, local_sem.at[2])
+    own_p = pltpu.make_async_copy(plan_in, plan, local_sem.at[3])
+    for copy in (own_f, own_t, own_c, own_p):
+        copy.start()
     pl.semaphore_wait(barrier, len(paths) + N_AUX - 1)
 
     groups = cut_rows(depth)
     pieces = [piece for group in groups for piece in group]
     held = depth // 2
+    right = (right_a, right_b)
     mine = pl.ds(pl.multiple_of(k * share, share), share)
 
     def send_piece(i, path, peer, src, slot):
@@ -188,8 +195,8 @@
         start(send_amp(path, peer, amp_in.at[mine], slot))
     send_own(0)
     send_own(1)
-    send_own(2)
     if not relayed:
+        send_own(2)
         send_own(3)
 
     @pl.loop(0, blocks)
@@ -212,7 +219,7 @@
                 ]
         swapped = jnp.dot(x, swap[...], preferred_element_type=jnp.float32)
         for s in range(SPREAD):
-            right[part_of, slot, s, span, :] = roll_groups(swapped, s * VB).astype(jnp.bfloat16)
+            right[part_of][slot, s, span, :] = roll_groups(swapped, s * VB).astype(jnp.bfloat16)
 
     def prepare_amp(slot):
         ampt[slot] = jnp.dot(
@@ -232,8 +239,8 @@
     def arrived(slot, i):
         send_piece(i, 0, t, fac_in, slot).wait_recv()
 
-    own_t.wait()
-    own_f.wait()
+    for copy in (own_f, own_t, own_c, own_p):
+        copy.wait()
     prepare_amp(RADIUS)
     for b in range(len(groups)):
         prepare(RADIUS, b)
@@ -250,15 +257,15 @@
             arrived(ahead, i)
             if relayed:
                 start(send_piece(i, 3, mate, fac.at[ahead], relay_to))
+                if i == 3:
+                    send_own(2)
             i += 1
         prepare(ahead, b)
         for j in range(i - len(group), i):
             arrived(near, j)
         prepare(near, b)
-        if b == 0:
-            amp_arrived(late, 3)
         if b == 1:
-            for slot in (ahead, near, behind, late):
+            for slot in (ahead, near, behind):
                 amp_ready(slot)
 
     lane_blocks = blocks // STEP
@@ -266,10 +273,11 @@
     def product(part_of, slot, s, cols):
         return jnp.dot(
             lt[part_of, plan[0, 0, slot], s],
-            right[part_of, plan[1, 0, slot], s, :, cols],
+            right[part_of][plan[1, 0, slot], s, :, cols],
             preferred_element_type=jnp.float32,
         )
 
+    amp_arrived(late, 3)
     i = 0
     for b, group in enumerate(groups):
         for slot in (behind, late):
@@ -277,6 +285,8 @@
                 arrived(slot, j)
             prepare(slot, b)
         i += len(group)
+        if b == 0:
+            amp_ready(late)
         if (b + 1) * LANES == held:
 
             @pl.loop(0, MOST)
@@ -287,14 +297,13 @@
                     for s in range(SPREAD):
                         vacc[slot, s, :, cols] = product(0, slot, s, cols)
 
-    tile = right.at[0]
+    tile = right_a
     height = blocks * VB
     group_of = lax.broadcasted_iota(jnp.int32, (height, LANES), 1) // VB
     is_odd = (group_of % 2).astype(jnp.float32).astype(jnp.bfloat16) > 0.5
     is_high = group_of.astype(jnp.float32).astype(jnp.bfloat16) > 1.5
 
-    @pl.loop(0, MOST)
-    def _(slot):
+    def finish(slot):
         for step in range(lane_blocks):
             outs = []
             for s in range(SPREAD):
@@ -315,6 +324,11 @@
                         tile[slot, row // height, at, hi * LANES : (hi + 1) * LANES] = mixed[
                             hi * VB : (hi + 1) * VB, :
                         ]
+
+    @pl.loop(0, MOST // PAIR)
+    def _(i):
+        for n in range(PAIR):
+            finish(i * PAIR + n)
 
     low = k % 2
     high = k // 2
@@ -361,22 +375,24 @@
     occ = amplitudes.shape[0]
     width = pairs // N_AUX
     n_pieces = sum(len(group) for group in cut_rows(depth))
-    anywhere = pl.BlockSpec(memory_space=pl.ANY)
-    scalars = pl.BlockSpec(memory_space=pltpu.SMEM)
+    anywhere = pl.BlockSpec(memory_space=pltpu.HBM)
     dma = pltpu.SemaphoreType.DMA
     return pl.pallas_call(
         functools.partial(kernel, n_task, relayed),
-        out_shape=jax.ShapeDtypeStruct((occ, width), jnp.float32),
-        in_specs=[scalars, scalars, anywhere, anywhere],
+        out_shape=pltpu.VMEM((occ, width), jnp.float32),
+        in_specs=[anywhere] * 4,
         out_specs=pl.BlockSpec(memory_space=pltpu.VMEM),
         scratch_shapes=[
             pltpu.VMEM((SPAN, depth, pairs), jnp.bfloat16),
             pltpu.VMEM((SPAN, occ, pairs), jnp.bfloat16),
+            pltpu.VMEM((SPAN, SPREAD, depth // 2, pairs), jnp.bfloat16),
             pltpu.VMEM((2, 2, occ, width), jnp.float32),
             pltpu.VMEM((2, occ, width), jnp.float32),
             pltpu.VMEM((occ, width), jnp.float32),
             pltpu.VMEM((occ, width), jnp.float32),
-            dma((2,)),
+            pltpu.SMEM(counts.shape, jnp.int32),
+            pltpu.SMEM(plan.shape, jnp.int32),
+            dma((4,)),
             dma((4, n_pieces)),
             dma((SPAN, n_pieces)),
             dma((4,)),

time: 79.8 us -> 74.4 us (0.932)
  Pallas kernels: 77.3 us -> 72.9 us
  local copies, waits for them, and re-layouts: 1.67 us -> 0.71 us
    pallas_call x1, Pallas kernels: 77.3 us -> 72.9 us  [run(): pl.pallas_call(functools.partial(kernel, n_task, relayed), out_shape=pltp...]
    unnamed x1, local copies, waits for them, and re-layouts: 1.67 us -> 0.71 us
where the time goes in v4:
time: 74.4 us; the launch traced here: 74.3 us
  Pallas kernels  72.9 us (98%)
    pallas_call x1, Pallas kernels, run(): pl.pallas_call(functools.partial(kernel, n_task, relayed), out_shape=pltp...  72.9 us

profile of v4, /device:TPU:1, one launch (start us, length us, event | category | flops | bytes accessed | tf_op | source)
XLA Modules:
  0.0 74.3 jit_solution(819746032733574451)
XLA Ops:
  0.7 72.9 %shard_map.46 = f32[256,256]{1,0:T(8,128)S(1)} custom-call(s32[1]{0:T(128)S(6)} %copy.7.counts_in, s32[3,1,4]{2,1,0:T(1,128)} %bitcast.7, bf16[512,1024]{1,0:T(8,128)(2,1)} %bitcast.5, bf16[256,1024]{1,0:T(8,128)(2,1)} %bitcast.6), custom_call_target="tpu_custom_call" | custom-call | tf_op jit(solution)/shard_map/pallas_call | solution.py:380
  73.6 0.7 copy.6

commit v5 on v4

--- a/solution.py
+++ b/solution.py
@@ -388,8 +388,8 @@
             pltpu.VMEM((SPAN, SPREAD, depth // 2, pairs), jnp.bfloat16),
             pltpu.VMEM((2, 2, occ, width), jnp.float32),
             pltpu.VMEM((2, occ, width), jnp.float32),
-            pltpu.VMEM((occ, width), jnp.float32),
-            pltpu.VMEM((occ, width), jnp.float32),
+            pltpu.VMEM((occ, width), jnp.bfloat16),
+            pltpu.VMEM((occ, width), jnp.bfloat16),
             pltpu.SMEM(counts.shape, jnp.int32),
             pltpu.SMEM(plan.shape, jnp.int32),
             dma((4,)),

time: 74.4 us -> 71.6 us (0.962)
  Pallas kernels: 72.9 us -> 70.1 us
    pallas_call x1, Pallas kernels: 72.9 us -> 70.1 us  [run(): pl.pallas_call(functools.partial(kernel, n_task, relayed), out_shape=pltp...]
where the time goes in v5:
time: 71.6 us; the launch traced here: 71.5 us
  Pallas kernels  70.1 us (98%)
    pallas_call x1, Pallas kernels, run(): pl.pallas_call(functools.partial(kernel, n_task, relayed), out_shape=pltp...  70.1 us

profile of v5, /device:TPU:1, one launch (start us, length us, event | category | flops | bytes accessed | tf_op | source)
XLA Modules:
  0.0 71.5 jit_solution(10166095697468035954)
XLA Ops:
  0.7 70.1 %shard_map.46 = f32[256,256]{1,0:T(8,128)S(1)} custom-call(s32[1]{0:T(128)S(6)} %copy.7.counts_in, s32[3,1,4]{2,1,0:T(1,128)} %bitcast.7, bf16[512,1024]{1,0:T(8,128)(2,1)} %bitcast.5, bf16[256,1024]{1,0:T(8,128)(2,1)} %bitcast.6), custom_call_target="tpu_custom_call" | custom-call | tf_op jit(solution)/shard_map/pallas_call | solution.py:380
  70.8 0.7 copy.6

commit v6 on v5

--- a/solution.py
+++ b/solution.py
@@ -15,7 +15,6 @@
 SPREAD = LANES // VB
 STEP = 2
 N_AUX = 4
-PAIR = 2
 MESH = pl.DeviceIdType.MESH
 
 
@@ -52,7 +51,8 @@
     pl.run_scoped(
         body,
         ampt=pltpu.VMEM((SPAN, occ, pairs), jnp.bfloat16),
-        lt=pltpu.VMEM((2, SPAN, SPREAD, rows, depth // 2), jnp.bfloat16),
+        lt_a=pltpu.VMEM((SPAN, SPREAD, rows, depth // 2), jnp.bfloat16),
+        lt_b=pltpu.VMEM((SPAN, SPREAD, rows, depth // 2), jnp.bfloat16),
         right_a=pltpu.VMEM((SPAN, SPREAD, depth // 2, pairs), jnp.bfloat16),
         vacc=pltpu.VMEM((MOST, SPREAD, rows, pairs), jnp.float32),
         swap=pltpu.VMEM((pairs, pairs), jnp.bfloat16),
@@ -86,7 +86,8 @@
     csend,
     crecv,
     ampt,
-    lt,
+    lt_a,
+    lt_b,
     right_a,
     vacc,
     swap,
@@ -146,6 +147,7 @@
     groups = cut_rows(depth)
     pieces = [piece for group in groups for piece in group]
     held = depth // 2
+    left = (lt_a, lt_b)
     right = (right_a, right_b)
     mine = pl.ds(pl.multiple_of(k * share, share), share)
 
@@ -207,19 +209,24 @@
         hit = rows == (cols % VB) * VB + cols // VB
         swap[pl.ds(base, LANES), :] = hit.astype(jnp.float32).astype(jnp.bfloat16)
 
-    def prepare(slot, b):
-        x = fac[slot, pl.ds(b * LANES, LANES), :]
+    def prepare(slots, b):
         part_of, lo = b * LANES // held, b * LANES % held
         span = pl.ds(lo, LANES)
-        for hi in range(blocks):
-            strip = x[:, hi * LANES : (hi + 1) * LANES].T
+        tiles = [fac[slot, pl.ds(b * LANES, LANES), :] for slot in slots]
+        for slot, x in zip(slots, tiles):
+            for hi in range(blocks):
+                strip = x[:, hi * LANES : (hi + 1) * LANES].T
+                for s in range(SPREAD):
+                    left[part_of][slot, s, hi * VB : (hi + 1) * VB, span] = strip[
+                        s * VB : (s + 1) * VB, :
+                    ]
+        swapped = jnp.dot(
+            jnp.concatenate(tiles, axis=0), swap[...], preferred_element_type=jnp.float32
+        )
+        for n, slot in enumerate(slots):
+            rows = swapped[n * LANES : (n + 1) * LANES, :]
             for s in range(SPREAD):
-                lt[part_of, slot, s, hi * VB : (hi + 1) * VB, span] = strip[
-                    s * VB : (s + 1) * VB, :
-                ]
-        swapped = jnp.dot(x, swap[...], preferred_element_type=jnp.float32)
-        for s in range(SPREAD):
-            right[part_of][slot, s, span, :] = roll_groups(swapped, s * VB).astype(jnp.bfloat16)
+                right[part_of][slot, s, span, :] = roll_groups(rows, s * VB).astype(jnp.bfloat16)
 
     def prepare_amp(slot):
         ampt[slot] = jnp.dot(
@@ -243,7 +250,7 @@
         copy.wait()
     prepare_amp(RADIUS)
     for b in range(len(groups)):
-        prepare(RADIUS, b)
+        prepare([RADIUS], b)
 
     amp_arrived(ahead, 0)
     if relayed:
@@ -260,19 +267,19 @@
                 if i == 3:
                     send_own(2)
             i += 1
-        prepare(ahead, b)
+        prepare([ahead], b)
         for j in range(i - len(group), i):
             arrived(near, j)
-        prepare(near, b)
+        prepare([near], b)
         if b == 1:
             for slot in (ahead, near, behind):
                 amp_ready(slot)
 
     lane_blocks = blocks // STEP
 
-    def product(part_of, slot, s, cols):
+    def product(part_of, slot, s, rows, cols):
         return jnp.dot(
-            lt[part_of, plan[0, 0, slot], s],
+            left[part_of][plan[0, 0, slot], s, rows],
             right[part_of][plan[1, 0, slot], s, :, cols],
             preferred_element_type=jnp.float32,
         )
@@ -283,7 +290,7 @@
         for slot in (behind, late):
             for j in range(i, i + len(group)):
                 arrived(slot, j)
-            prepare(slot, b)
+        prepare([behind, late], b)
         i += len(group)
         if b == 0:
             amp_ready(late)
@@ -295,20 +302,22 @@
                 def _(step):
                     cols = pl.ds(pl.multiple_of(step * lanes, lanes), lanes)
                     for s in range(SPREAD):
-                        vacc[slot, s, :, cols] = product(0, slot, s, cols)
+                        vacc[slot, s, :, cols] = product(0, slot, s, slice(None), cols)
 
     tile = right_a
     height = blocks * VB
-    group_of = lax.broadcasted_iota(jnp.int32, (height, LANES), 1) // VB
+    half = height // 2
+    group_of = lax.broadcasted_iota(jnp.int32, (half, LANES), 1) // VB
     is_odd = (group_of % 2).astype(jnp.float32).astype(jnp.bfloat16) > 0.5
     is_high = group_of.astype(jnp.float32).astype(jnp.bfloat16) > 1.5
 
-    def finish(slot):
+    def finish(side, slot):
+        rows = pl.ds(pl.multiple_of(side * half, half), half)
         for step in range(lane_blocks):
             outs = []
             for s in range(SPREAD):
                 cols = pl.ds(step * lanes, lanes)
-                whole = vacc[slot, s, :, cols] + product(1, slot, s, cols)
+                whole = vacc[slot, s, rows, cols] + product(1, slot, s, rows, cols)
                 outs.append(whole.astype(jnp.bfloat16))
             for j in range(STEP):
                 x = [o[:, j * LANES : (j + 1) * LANES] for o in outs]
@@ -320,15 +329,11 @@
                         mixed = pltpu.roll(mixed, LANES - d * VB, 1)
                     row = ((step * STEP + j) * SPREAD + d) * VB
                     at = pl.ds(row % height, VB)
-                    for hi in range(blocks):
-                        tile[slot, row // height, at, hi * LANES : (hi + 1) * LANES] = mixed[
+                    for hi in range(half // VB):
+                        base = pl.multiple_of(side * 2 * width + hi * LANES, LANES)
+                        tile[slot, row // height, at, pl.ds(base, LANES)] = mixed[
                             hi * VB : (hi + 1) * VB, :
                         ]
-
-    @pl.loop(0, MOST // PAIR)
-    def _(i):
-        for n in range(PAIR):
-            finish(i * PAIR + n)
 
     low = k % 2
     high = k // 2
@@ -343,28 +348,39 @@
             device_id_type=MESH,
         )
 
-    for stage, side in enumerate((1 - high, high)):
-        cols = pl.ds(pl.multiple_of(side * 2 * width, 2 * width), 2 * width)
-        total = jnp.zeros((occ, 2 * width), jnp.float32)
+    def terms(base, size):
+        cols = pl.ds(pl.multiple_of(base, width), size)
+        total = jnp.zeros((occ, size), jnp.float32)
         for slot in range(MOST):
-            weights = tile[slot, :, :, cols].reshape(pairs, 2 * width)
+            weights = tile[slot, :, pl.ds(0, height), cols].reshape(pairs, size)
             term = jnp.dot(
                 ampt[plan[2, 0, slot]], weights, preferred_element_type=jnp.float32
             )
             total += jnp.where(slot < counts[0], term, 0.0)
-        part[stage, 0] = total[:, :width]
-        part[stage, 1] = total[:, width:]
-        pair = swap_sums(stage, 1, part.at[stage, 1 - low], inbox.at[stage])
-        start(pair)
-        if stage == 0:
-            pair.wait_recv()
-            xsend[...] = (part[stage, low] + inbox[stage]).astype(xsend.dtype)
-            far = swap_sums(2, 2, xsend, xin)
-            start(far)
-        else:
-            pair.wait_recv()
-            far.wait_recv()
-            out[...] = part[stage, low] + inbox[stage] + xin[...].astype(jnp.float32)
+        return total
+
+    other = 1 - high
+    for slot in range(MOST):
+        finish(other, slot)
+    total = terms(other * 2 * width, 2 * width)
+    part[0, 0] = total[:, :width]
+    part[0, 1] = total[:, width:]
+    pair = swap_sums(0, 1, part.at[0, 1 - low], inbox.at[0])
+    start(pair)
+    pair.wait_recv()
+    xsend[...] = (part[0, low] + inbox[0]).astype(xsend.dtype)
+    far = swap_sums(2, 2, xsend, xin)
+    start(far)
+    for slot in range(MOST):
+        finish(high, slot)
+    part[1, 0] = terms((high * 2 + 1 - low) * width, width)
+    pair = swap_sums(1, 1, part.at[1, 0], inbox.at[1])
+    start(pair)
+    kept = terms(k * width, width)
+    pair.wait_recv()
+    kept += inbox[1]
+    far.wait_recv()
+    out[...] = kept + xin[...].astype(jnp.float32)
 
     for copy in started:
         copy.wait_send()

time: 71.6 us -> 70.9 us (level)
  Pallas kernels: 70.1 us -> 68.9 us
    pallas_call x1, Pallas kernels: 70.1 us -> 68.9 us  [run(): pl.pallas_call(functools.partial(kernel, n_task, relayed), out_shape=pltp...]
where the time goes in v6:
time: 70.9 us; the launch traced here: 70.3 us
  Pallas kernels  68.9 us (97%)
  local copies, waits for them, and re-layouts  0.71 us (1%)
    pallas_call x1, Pallas kernels, run(): pl.pallas_call(functools.partial(kernel, n_task, relayed), out_shape=pltp...  68.9 us

profile of v6, /device:TPU:1, one launch (start us, length us, event | category | flops | bytes accessed | tf_op | source)
XLA Modules:
  0.0 70.3 jit_solution(9491688242839576433)
XLA Ops:
  0.7 68.9 %shard_map.46 = f32[256,256]{1,0:T(8,128)S(1)} custom-call(s32[1]{0:T(128)S(6)} %copy.7.counts_in, s32[3,1,4]{2,1,0:T(1,128)} %bitcast.7, bf16[512,1024]{1,0:T(8,128)(2,1)} %bitcast.5, bf16[256,1024]{1,0:T(8,128)(2,1)} %bitcast.6), custom_call_target="tpu_custom_call" | custom-call | tf_op jit(solution)/shard_map/pallas_call | solution.py:396
  69.6 0.7 %copy.6 = f32[1,256,256]{2,1,0:T(8,128)} copy(f32[1,256,256]{2,1,0:T(8,128)S(1)} %bitcast.4) | data formatting | bytes 524288
